TPU v7x, 32 devices: a whole 2x2x4 slice. The times are simulated.
32 devices in a mesh: group: 2 (over x), dp: 2 (over core), tensor: 8 (over z, y).
Axes of the slice: x: 2, y: 2, z: 4, core: 2. Of those that a mesh axis runs over, the one named last changes fastest.
Arguments:
- teacher_hidden: bfloat16 [1024, 8192], P(('group', 'dp'), 'tensor'), may hold values from -6 to 6
- teacher_gain: float32 [8192], P('tensor'), may hold values from 0.1 to 1.9
- project_weight: bfloat16 [8192, 3584], P('tensor'), may hold values from -0.0625 to 0.0625
- student_hidden: bfloat16 [1024, 3584], P(('group', 'dp', 'tensor')), may hold values from -6 to 6
- student_gain: float32 [3584], replicated, may hold values from 0.1 to 1.9
- gate_weight: bfloat16 [3584, 9472], P(('group', 'dp'), 'tensor'), may hold values from -0.09375 to 0.09375
- up_weight: bfloat16 [3584, 9472], P(('group', 'dp'), 'tensor'), may hold values from -0.09375 to 0.09375
- down_weight: bfloat16 [9472, 3584], P('tensor', ('group', 'dp')), may hold values from -0.0625 to 0.0625
- owner_map: int32 [64, 1], P(('group', 'dp')), may hold values from 0 to 3; in each aligned block of 16 rows (0 to 15, 16 to 31, ...) at most 8 rows name the same one
- token_ids: int32 [1024], P(('group', 'dp', 'tensor')), may hold values from 0 to 511
- token_counts: int32 [64], P(('group', 'dp')), may hold values from 1 to 16
- id_weight: float32 [512], replicated, may hold values from 0.25 to 4
Outputs:
- student_out: bfloat16 [4, 16, 32, 3584], P(('group', 'dp'), 'tensor')
- down_grad: float32 [3584, 9472], P(('group', 'dp'), 'tensor')
Inputs may be any that keep to these rules, and one draw needn't show every extreme that they name: `owner_map`: of the 16 episodes of one index of group and dp (aligned blocks of 16 rows), at most 8 have the same owner; owner o is index o of group and dp in mesh order.
All inputs are finite; a program needn't handle non-finite values.
Results may differ from a plain program's by a relative error of at most 0.02.
Values may be sent and summed in bfloat16 or wider, within the bound.
A program may use at most 128 MiB of HBM per device.

v0:
```python
import math
import jax
import jax.numpy as jnp
from jax import lax
from jax.sharding import PartitionSpec as P

EP_LEN = 16
EXTRA = 128
EPSILON = 1e-06
OWNER_AXES = ("group", "dp")


def exchange(blocks):
    return lax.all_to_all(blocks, OWNER_AXES, split_axis=0, concat_axis=0, tiled=True)


def by_columns(rows, owners):
    return rows.reshape(rows.shape[0], owners, -1).transpose(1, 0, 2)


def three_terms(values):
    high = lax.reduce_precision(values, 8, 7)
    rest = values - high
    middle = lax.reduce_precision(rest, 8, 7)
    return (high, middle, rest - middle)


def build_selector(owner_list, owners, capacity):
    onehot = (owner_list[:, :, None] == jnp.arange(owners, dtype=jnp.int32)).astype(jnp.int32)
    earlier = jnp.cumsum(onehot, axis=1) - onehot
    rank_list = jnp.sum(earlier * onehot, axis=2)
    target = owner_list * capacity + rank_list
    slots = jnp.arange(owners * capacity, dtype=jnp.int32)
    return (target[:, None, :] == slots[None, :, None]).astype(jnp.bfloat16)


def local(
    teacher_hidden,
    teacher_gain,
    project_weight,
    student_hidden,
    student_gain,
    gate_weight,
    up_weight,
    down_weight,
    owner_map,
    token_ids,
    token_counts,
    id_weight,
):
    owners = lax.axis_size("group") * lax.axis_size("dp")
    tensors = lax.axis_size("tensor")
    tensor_index = lax.axis_index("tensor")
    owner_index = lax.axis_index(OWNER_AXES)
    episodes = token_counts.shape[0]
    own_span = EP_LEN // tensors
    share = own_span * episodes
    capacity = max(2, 2 * episodes // owners)
    received = owners * capacity
    student_width = student_hidden.shape[1]
    width = student_width // owners
    tokens_all = EP_LEN * episodes * owners
    teacher_width = teacher_hidden.shape[1] * tensors
    id_rows = token_ids.reshape(own_span, episodes)
    looked = jnp.sum(
        jnp.where(
            id_rows[:, :, None] == jnp.arange(id_weight.shape[0], dtype=jnp.int32)[None, None, :],
            id_weight[None, None, :],
            0.0,
        ),
        axis=2,
    )
    position = tensor_index * own_span + jnp.arange(own_span, dtype=jnp.int32)[:, None]
    token_weight = jnp.where(position < token_counts[None, :], looked, 0.0).reshape(share, 1)
    own_rows = student_hidden.astype(jnp.float32)
    own_rescale = lax.rsqrt(jnp.mean(own_rows * own_rows, axis=1, keepdims=True) + EPSILON)
    owner_rows = jnp.tile(owner_map.astype(jnp.float32), (own_span, 1))
    extras = jnp.concatenate([token_weight, owner_rows, *three_terms(own_rescale)], axis=1)
    extras = jnp.pad(extras, ((0, 0), (0, EXTRA - extras.shape[1]))).astype(jnp.bfloat16)
    arrived = exchange(
        jnp.concatenate(
            [
                by_columns(student_hidden, owners),
                jnp.broadcast_to(extras[None], (owners, share, EXTRA)),
            ],
            axis=2,
        )
    )
    rows = owners * share
    student_block = arrived[:, :, :width].reshape(rows, width).astype(jnp.float32)
    facts = arrived[:, :, width:].astype(jnp.float32)
    weight_rows = facts[:, :, 0].reshape(rows, 1)
    owner_list = facts[:, :episodes, 1].astype(jnp.int32)
    rescale = (facts[:, :, 2] + facts[:, :, 3] + facts[:, :, 4]).reshape(rows, 1)
    gain = lax.dynamic_slice_in_dim(student_gain, owner_index * width, width, 0)
    normed = (student_block * rescale * gain[None, :]).astype(jnp.bfloat16)
    gathered = lax.all_gather(normed, "tensor", axis=0, tiled=True)
    widened = teacher_hidden.astype(jnp.float32)
    squares = jnp.sum(widened * widened, axis=1)
    scaled = (widened * teacher_gain[None, :]).astype(jnp.bfloat16)
    inverse = lax.rsqrt(lax.psum(squares, "tensor") / teacher_width + EPSILON)
    summed = lax.psum_scatter(
        jnp.dot(scaled, project_weight, preferred_element_type=jnp.float32).astype(jnp.bfloat16),
        "tensor",
        scatter_dimension=0,
        tiled=True,
    ).astype(jnp.float32)
    own_inverse = lax.dynamic_slice_in_dim(inverse, tensor_index * share, share, 0)
    projected = exchange(by_columns((summed * own_inverse[:, None]).astype(jnp.bfloat16), owners))
    hidden = gate_weight.shape[1]
    gate_part = jnp.dot(gathered, gate_weight, preferred_element_type=jnp.float32)
    up_part = jnp.dot(gathered, up_weight, preferred_element_type=jnp.float32)
    parts = jnp.stack(
        [
            gate_part.astype(jnp.bfloat16).reshape(owners, -1, hidden),
            up_part.astype(jnp.bfloat16).reshape(owners, -1, hidden),
        ],
        axis=1,
    )
    sums = lax.psum_scatter(parts, OWNER_AXES, scatter_dimension=0, tiled=True).astype(jnp.float32)
    activated = (jax.nn.silu(sums[0, 0]) * sums[0, 1]).astype(jnp.bfloat16)
    act_all = lax.all_gather(activated, OWNER_AXES, axis=0, tiled=True)
    branch = jnp.dot(act_all, down_weight, preferred_element_type=jnp.float32)
    branch_local = lax.psum_scatter(
        branch.astype(jnp.bfloat16), "tensor", scatter_dimension=0, tiled=True
    ).astype(jnp.float32)
    predicted = student_block + branch_local
    difference = predicted - projected.reshape(rows, width).astype(jnp.float32)
    grad_block = (weight_rows * difference * (1.0 / math.sqrt(tokens_all))).astype(jnp.bfloat16)
    grad_all = lax.all_gather(grad_block, "tensor", axis=0, tiled=True)
    down_grad = jnp.einsum("rc,rh->ch", grad_all, act_all, preferred_element_type=jnp.float32)
    selector = build_selector(owner_list, owners, capacity)
    picked = jnp.einsum(
        "sre,spef->sprf",
        selector,
        predicted.astype(jnp.bfloat16).reshape(owners, own_span, episodes, width),
        preferred_element_type=jnp.float32,
    ).astype(jnp.bfloat16)
    outgoing = picked.reshape(owners, own_span, owners, capacity, width).transpose(2, 1, 0, 3, 4)
    incoming = exchange(outgoing.reshape(owners, own_span, received, width))
    student_out = incoming.transpose(1, 2, 0, 3).reshape(1, own_span, received, student_width)
    return (student_out, down_grad)


def solution(mesh):
    in_specs = (
        P(("group", "dp"), "tensor"),
        P("tensor"),
        P("tensor", None),
        P(("group", "dp", "tensor"), None),
        P(),
        P(("group", "dp"), "tensor"),
        P(("group", "dp"), "tensor"),
        P("tensor", ("group", "dp")),
        P(("group", "dp"), None),
        P(("group", "dp", "tensor")),
        P(("group", "dp")),
        P(),
    )
    out_specs = (P(("group", "dp"), "tensor", None, None), P(("group", "dp"), "tensor"))
    return jax.shard_map(local, mesh=mesh, in_specs=in_specs, out_specs=out_specs, check_vma=False)
```

profile of v0, /device:TPU:0, one launch (start us, length us, event | category | flops | bytes accessed | tf_op | source)
XLA Modules:
  0.0 378.6 jit_solution(4953372782439392148)
XLA Ops:
  7.2 0.0 copy-start
  7.2 1.2 multiply_reduce_fusion
  8.4 1.0 reshape.158
  9.4 0.7 eq.43
  10.2 0.8 select_reduce_fusion
  11.0 0.7 fusion.19
  11.8 0.1 select_n.26
  11.9 0.7 convert_bitcast_fusion
  12.5 0.1 tile.13
  12.6 0.1 copy.50
  12.8 0.7 pad_maximum_fusion.1
  13.5 4.2 %all-to-all-start = ((bf16[4,32,1024]{2,1,0:T(8,128)(2,1)}), bf16[4,32,1024]{2,1,0:T(8,128)(2,1)S(1)}, u32[]{:S(2)}, u32[]{:S(2)}) async-start(bf16[4,32,1024]{2,1,0:T(8,128)(2,1)} %pad_maximum_fusion.1), calls=%async_computation | async-start | bytes 524288 | tf_op jit(solution)/shard_map/all_to_all | solution.py:14
  17.8 0.8 dynamic_slice.6
  18.6 5.2 %all-to-all-done = bf16[4,32,1024]{2,1,0:T(8,128)(2,1)S(1)} async-done(((bf16[4,32,1024]{2,1,0:T(8,128)(2,1)}), bf16[4,32,1024]{2,1,0:T(8,128)(2,1)S(1)}, u32[]{:S(2)}, u32[]{:S(2)}) %all-to-all-start) | async-done | bytes 262176 | tf_op jit(solution)/shard_map/all_to_all | solution.py:14
  23.8 0.2 slice_reduce_fusion
  24.0 0.1 add.97
  24.1 0.8 fusion.8
  24.9 0.0 all-gather.4.cloned.1.call-update
  25.0 0.0 reduce-scatter.4.cloned.1.call-start
  25.0 47.4 %all-gather.4.cloned.1.call-done = bf16[1024,896]{1,0:T(8,128)(2,1)} async-done(((bf16[128,896]{1,0:T(8,128)(2,1)}), bf16[1024,896]{1,0:T(8,128)(2,1)}) %all-gather.4.cloned.1.call-update) | async-done | bytes 1835024 | tf_op jit(solution)/shard_map/all_gather | solution.py:97
  72.4 5.5 %convolution_convert_fusion.2 = bf16[1024,1184]{0,1:T(8,128)(2,1)} fusion(bf16[1024,896]{1,0:T(8,128)(2,1)} %all-gather.4.cloned.1.call-done, bf16[896,1184]{0,1:T(8,128)(2,1)S(1)} %copy-done), kind=kOutput, calls=%fused_computation.3 | convolution fusion | flops 2173861888 | bytes 6381568 | tf_op jit(solution)/shard_map/dot_general | solution.py:111
  77.9 5.7 %stack_reshape.6 = bf16[4,1,256,1184]{2,0,3,1:T(4,128)(2,1)} reshape(bf16[1024,1184]{0,1:T(8,128)(2,1)} %convolution_convert_fusion.2) | data formatting | bytes 4849664 | tf_op jit(solution)/shard_map/stack;reshape | solution.py:113
  83.6 3.6 copy.44
  87.2 4.0 %convolution_convert_fusion.1 = bf16[1024,1184]{0,1:T(8,128)(2,1)} fusion(bf16[1024,896]{1,0:T(8,128)(2,1)S(1)} %copy-done.4, bf16[896,1184]{0,1:T(8,128)(2,1)S(1)} %copy-done.3), kind=kOutput, calls=%fused_computation.2 | convolution fusion | flops 2173861888 | bytes 6381568 | tf_op jit(solution)/shard_map/dot_general | solution.py:112
  91.2 5.7 %stack_reshape.7 = bf16[4,1,256,1184]{2,0,3,1:T(4,128)(2,1)} reshape(bf16[1024,1184]{0,1:T(8,128)(2,1)} %convolution_convert_fusion.1) | data formatting | bytes 4849664 | tf_op jit(solution)/shard_map/stack;reshape | solution.py:113
  96.9 2.1 copy.45
  99.0 0.3 copy-done.1
  99.3 2.6 pad_maximum_fusion
  101.9 0.0 reduce-scatter.4.cloned.1.call-update
  101.9 0.0 all-gather.6.cloned.1.call-start
  102.0 47.6 %reduce-scatter.4.cloned.1.call-done = bf16[1,2,256,1184]{2,3,1,0:T(8,128)(2,1)} async-done(((bf16[4,2,256,1184]{2,3,1,0:T(8,128)(2,1)}), bf16[1,2,256,1184]{2,3,1,0:T(8,128)(2,1)}) %reduce-scatter.4.cloned.1.call-update) | async-done | bytes 1212432 | tf_op jit(solution)/shard_map/reduce_scatter | solution.py:120
  149.6 1.4 convert_element_type.93
  151.1 1.2 fusion.2
  152.3 0.0 all-gather.6.cloned.1.call-update
  152.3 0.0 reduce-scatter.8.cloned.1.call-start
  152.3 6.4 %convolution_convert_fusion = bf16[256,3584]{1,0:T(8,128)(2,1)} fusion(bf16[1024,3584]{1,0:T(8,128)(2,1)} %param.14, bf16[256,1024]{1,0:T(8,128)(2,1)S(1)} %copy-done.2, f32[1024]{0:T(1024)S(1)} %copy-done.5), kind=kOutput, calls=%fused_computation | convolution fusion | flops 1880752128 | bytes 9703424 | tf_op jit(solution)/shard_map/dot_general | solution.py:103
  158.7 0.0 reduce-scatter.8.cloned.1.call-update
  158.7 0.0 reduce-scatter.6.cloned.1.call-start
  158.8 18.4 %all-gather.6.cloned.1.call-done = bf16[1024,1184]{0,1:T(8,128)(2,1)} async-done(((bf16[256,1184]{0,1:T(8,128)(2,1)}), bf16[1024,1184]{0,1:T(8,128)(2,1)}) %all-gather.6.cloned.1.call-update) | async-done | bytes 2424848 | tf_op jit(solution)/shard_map/all_gather | solution.py:122
  177.1 6.5 %convolution_convert_fusion.3 = bf16[1024,896]{1,0:T(8,128)(2,1)} fusion(bf16[1024,1184]{0,1:T(8,128)(2,1)} %all-gather.6.cloned.1.call-done, bf16[1184,896]{1,0:T(8,128)(2,1)} %param.19), kind=kOutput, calls=%fused_computation.4 | convolution fusion | flops 2173566976 | bytes 6381568 | tf_op jit(solution)/shard_map/dot_general | solution.py:123
  183.6 0.0 reduce-scatter.6.cloned.1.call-update
  183.7 0.2 fusion.4
  183.8 21.4 %psum.7 = f32[256]{0:T(256)S(1)} all-reduce(f32[256]{0:T(256)S(1)} %fusion.4), channel_id=1, replica_groups=mesh['group'=2,'dp'=2,'tensor'=8] {'tensor'}, use_global_device_ids=true, to_apply=%region_8.9 | all-reduce | flops 256 | bytes 2048 | tf_op jit(solution)/shard_map/psum | solution.py:101
  205.2 0.1 dynamic_slice.7
  205.3 41.9 %reduce-scatter.8.cloned.1.call-done = bf16[32,3584]{1,0:T(8,128)(2,1)} async-done(((bf16[256,3584]{1,0:T(8,128)(2,1)}), bf16[32,3584]{1,0:T(8,128)(2,1)}) %reduce-scatter.8.cloned.1.call-update) | async-done | bytes 229392 | tf_op jit(solution)/shard_map/reduce_scatter | solution.py:102
  247.2 1.0 multiply_convert_fusion
  248.3 0.7 copy.55
  249.0 3.4 all-to-all-start.2
  252.4 0.2 all-gather.8.cloned.1.call-start
  252.6 0.1 mul.103
  252.7 5.3 %all-to-all-done.2 = bf16[4,32,896]{2,1,0:T(8,128)(2,1)S(1)} async-done(((bf16[4,32,896]{2,1,0:T(8,128)(2,1)}), bf16[4,32,896]{2,1,0:T(8,128)(2,1)S(1)}, u32[]{:S(2)}, u32[]{:S(2)}) %all-to-all-start.2) | async-done | bytes 229408 | tf_op jit(solution)/shard_map/all_to_all | solution.py:14
  258.0 58.9 %reduce-scatter.6.cloned.1.call-done = bf16[128,896]{1,0:T(8,128)(2,1)} async-done(((bf16[1024,896]{1,0:T(8,128)(2,1)}), bf16[128,896]{1,0:T(8,128)(2,1)}) %reduce-scatter.6.cloned.1.call-update) | async-done | bytes 229392 | tf_op jit(solution)/shard_map/reduce_scatter | solution.py:124
  316.8 1.8 fusion.11
  318.6 0.0 all-gather.8.cloned.1.call-update
  318.6 0.3 fusion.17
  318.9 0.1 fusion.14
  319.0 0.1 reduce_window_sum.11
  319.0 0.2 select_reduce_fusion.1
  319.3 0.4 fusion
  319.7 10.6 %all_to_all.15 = bf16[4,2,32,896]{3,2,1,0:T(8,128)(2,1)S(1)} all-to-all(bf16[4,2,32,896]{3,2,1,0:T(8,128)(2,1)S(1)} %bitcast.65), channel_id=1, replica_groups=mesh['group'=2,'dp'=2,'tensor'=8] {'group','dp'}, dimensions={0} | all-to-all | bytes 917504 | tf_op jit(solution)/shard_map/all_to_all | solution.py:14
  330.3 0.4 copy.47
  330.7 0.9 reshape.162
  331.6 33.1 %all-gather.8.cloned.1.call-done = bf16[1024,896]{1,0:T(8,128)(2,1)} async-done(((bf16[128,896]{1,0:T(8,128)(2,1)}), bf16[1024,896]{1,0:T(8,128)(2,1)}) %all-gather.8.cloned.1.call-update) | async-done | bytes 1835024 | tf_op jit(solution)/shard_map/all_gather | solution.py:130
  364.8 6.9 %fusion.21 = f32[896,1184]{0,1:T(8,128)} fusion(bf16[1024,1184]{0,1:T(8,128)(2,1)} %all-gather.6.cloned.1.call-done, bf16[1024,896]{1,0:T(8,128)(2,1)} %all-gather.8.cloned.1.call-done), kind=kOutput, calls=%fused_computation.57 | convolution fusion | flops 2172649472 | bytes 8503296 | tf_op jit(solution)/shard_map/rc,rh->ch/dot_general | solution.py:131
  (23 shorter events, 0.2 us)
Async XLA Ops:
  7.2 65.3 %copy-start = (bf16[896,1184]{0,1:T(8,128)(2,1)S(1)}, bf16[896,1184]{0,1:T(8,128)(2,1)}, u32[]{:S(2)}) copy-start(bf16[896,1184]{0,1:T(8,128)(2,1)} %param.17) | copy-start | bytes 6365188
  13.5 10.2 %all-to-all-start = ((bf16[4,32,1024]{2,1,0:T(8,128)(2,1)}), bf16[4,32,1024]{2,1,0:T(8,128)(2,1)S(1)}, u32[]{:S(2)}, u32[]{:S(2)}) async-start(bf16[4,32,1024]{2,1,0:T(8,128)(2,1)} %pad_maximum_fusion.1), calls=%async_computation | async-start | bytes 524288 | tf_op jit(solution)/shard_map/all_to_all | solution.py:14
  17.8 54.7 %all-gather.4.cloned.1.call-start = ((), (), s32[]{:S(2)}) async-start(), calls=%async_computation.6 | async-start | bytes 2064384 | tf_op jit(solution)/shard_map/all_gather | solution.py:97
  25.0 124.6 %reduce-scatter.4.cloned.1.call-start = ((), (), s32[]{:S(2)}) async-start(), calls=%async_computation.7 | async-start | bytes 6062080 | tf_op jit(solution)/shard_map/reduce_scatter | solution.py:120
  83.6 3.6 copy-start.3
  83.6 3.6 copy-start.4
  96.9 2.4 copy-start.1
  101.9 75.2 %all-gather.6.cloned.1.call-start = ((), (), s32[]{:S(2)}) async-start(), calls=%async_computation.8 | async-start | bytes 3031040 | tf_op jit(solution)/shard_map/all_gather | solution.py:122
  151.0 1.3 copy-start.2
  151.1 1.3 copy-start.5
  152.3 94.9 %reduce-scatter.8.cloned.1.call-start = ((), (), s32[]{:S(2)}) async-start(), calls=%async_computation.10 | async-start | bytes 2064384 | tf_op jit(solution)/shard_map/reduce_scatter | solution.py:102
  158.7 158.1 %reduce-scatter.6.cloned.1.call-start = ((), (), s32[]{:S(2)}) async-start(), calls=%async_computation.9 | async-start | bytes 2064384 | tf_op jit(solution)/shard_map/reduce_scatter | solution.py:124
  249.0 9.0 %all-to-all-start.2 = ((bf16[4,32,896]{2,1,0:T(8,128)(2,1)}), bf16[4,32,896]{2,1,0:T(8,128)(2,1)S(1)}, u32[]{:S(2)}, u32[]{:S(2)}) async-start(bf16[4,32,896]{2,1,0:T(8,128)(2,1)} %bitcast.64), calls=%async_computation.5 | async-start | bytes 458752 | tf_op jit(solution)/shard_map/all_to_all | solution.py:14
  252.4 112.4 %all-gather.8.cloned.1.call-start = ((), (), s32[]{:S(2)}) async-start(), calls=%async_computation.11 | async-start | bytes 2064384 | tf_op jit(solution)/shard_map/all_gather | solution.py:130
Sparse Core Ops, SparseCore 0:
  25.1 47.3 all-gather.3
  102.0 47.4 reduce-scatter.3
  152.4 24.7 all-gather.5
  180.5 66.7 reduce-scatter.7
  251.1 65.6 reduce-scatter.5
  319.5 45.2 all-gather.7
where the time goes:
time: 379 us
  waiting for transfers between devices  258 us (68%)
  blocking collectives  32 us (8%)
  matrix products  29.6 us (8%)
  local copies, waits for them, and re-layouts  22.6 us (6%)
  between operations  14.3 us (4%)
  other arithmetic  14.1 us (4%)
  starting transfers between devices  8.01 us (2%)
    reduce_scatter x1, waiting for transfers between devices, local(): lax.psum_scatter(branch.astype(jnp.bfloat16), 'tensor', scatter_dimension...  58.9 us
    reduce_scatter x1, waiting for transfers between devices, local(): lax.psum_scatter(parts, OWNER_AXES, scatter_dimension=0, tiled=True)  47.6 us
    all_gather x1, waiting for transfers between devices, local(): gathered = lax.all_gather(normed, 'tensor', axis=0, tiled=True)  47.4 us
    reduce_scatter x1, waiting for transfers between devices, local(): lax.psum_scatter(jnp.dot(scaled, project_weight, preferred_element_type=j...  41.9 us
    all_gather x1, waiting for transfers between devices, local(): grad_all = lax.all_gather(grad_block, 'tensor', axis=0, tiled=True)  33.1 us
    psum x1, blocking collectives, local(): inverse = lax.rsqrt(lax.psum(squares, 'tensor') / teacher_width + EPSILON)  21.4 us
    all_gather x1, waiting for transfers between devices, local(): act_all = lax.all_gather(activated, OWNER_AXES, axis=0, tiled=True)  18.4 us
    another operation x4, local copies, waits for them, and re-layouts, local(): jnp.stack([gate_part.astype(jnp.bfloat16).reshape(owners, -1, hidden), up...  17.2 us
  transfers between devices with their start and end apart: 8, of which 8 were waited for; matrix products, arithmetic and copies ran while one was open for 5% of the time, Pallas kernels for 0%

commit v1 on v0

--- a/solution.py
+++ b/solution.py
@@ -8,6 +8,25 @@
 EXTRA = 128
 EPSILON = 1e-06
 OWNER_AXES = ("group", "dp")
+
+
+def _answer_units(m, local_values):
+    along_axis = "tensor"
+    n_now, left_arr, u1 = (
+        jax.lax.axis_size(along_axis),
+        jax.lax.axis_index(along_axis),
+        m.shape[0],
+    )
+    by_rank = [(ix, (ix + 1) % n_now) for ix in range(n_now)]
+    z1, x_next = (m, None)
+    for num in range(n_now):
+        lower = (
+            jax.lax.ppermute(z1, axis_name=along_axis, perm=by_rank) if num < n_now - 1 else None
+        )
+        state_next = local_values(z1, (left_arr - num) % n_now * u1)
+        x_next = state_next if x_next is None else x_next + state_next
+        z1 = lower
+    return x_next
 
 
 def exchange(blocks):
@@ -127,8 +146,15 @@
     predicted = student_block + branch_local
     difference = predicted - projected.reshape(rows, width).astype(jnp.float32)
     grad_block = (weight_rows * difference * (1.0 / math.sqrt(tokens_all))).astype(jnp.bfloat16)
-    grad_all = lax.all_gather(grad_block, "tensor", axis=0, tiled=True)
-    down_grad = jnp.einsum("rc,rh->ch", grad_all, act_all, preferred_element_type=jnp.float32)
+    down_grad = _answer_units(
+        grad_block,
+        lambda shard, start: jnp.einsum(
+            "rc,rh->ch",
+            shard,
+            lax.dynamic_slice_in_dim(act_all, start, shard.shape[0], axis=0),
+            preferred_element_type=jnp.float32,
+        ),
+    )
     selector = build_selector(owner_list, owners, capacity)
     picked = jnp.einsum(
         "sre,spef->sprf",

time: 379 us -> 397 us (1.047)
  waiting for transfers between devices: 258 us -> 275 us
  blocking collectives: 32 us -> 21.5 us
  matrix products: 29.6 us -> 36.6 us
  starting transfers between devices: 8.01 us -> 12.3 us
    ppermute x0 -> x7, waiting for transfers between devices: none -> 51.1 us  [_answer_units(): jax.lax.ppermute(z1, axis_name=along_axis, perm=by_rank)]
    all_gather x1 -> x0, waiting for transfers between devices: 33.1 us -> none  [local(): grad_all = lax.all_gather(grad_block, 'tensor', axis=0, tiled=True)]
    all_to_all x1 -> x0, blocking collectives: 10.6 us -> none  [exchange(): lax.all_to_all(blocks, OWNER_AXES, split_axis=0, concat_axis=0, tiled=True)]
    dot_general x1 -> x8, matrix products: 6.93 us -> 13.9 us  [local(): jnp.einsum('rc,rh->ch', shard, lax.dynamic_slice_in_dim(act_all, start, s...]
    all_to_all x2 -> x3, starting transfers between devices: 7.62 us -> 11.3 us  [exchange(): lax.all_to_all(blocks, OWNER_AXES, split_axis=0, concat_axis=0, tiled=True)]
    all_to_all x2 -> x3, waiting for transfers between devices: 10.5 us -> 10.2 us  [exchange(): lax.all_to_all(blocks, OWNER_AXES, split_axis=0, concat_axis=0, tiled=True)]
  transfers between devices with their start and end apart: 8 -> 15, of which waited for: 8 -> 14; matrix products, arithmetic and copies ran while one was open for 5% -> 7% of each run, Pallas kernels for 0% -> 0%
where the time goes in v1:
time: 397 us; the launch traced here: 396 us
  waiting for transfers between devices  275 us (69%)
  matrix products  36.6 us (9%)
  local copies, waits for them, and re-layouts  23.4 us (6%)
  blocking collectives  21.5 us (5%)
  between operations  14.1 us (4%)
  other arithmetic  13.4 us (3%)
  starting transfers between devices  12.3 us (3%)
    reduce_scatter x1, waiting for transfers between devices, local(): lax.psum_scatter(branch.astype(jnp.bfloat16), 'tensor', scatter_dimension...  58.7 us
    ppermute x7, waiting for transfers between devices, _answer_units(): jax.lax.ppermute(z1, axis_name=along_axis, perm=by_rank)  51.1 us
    reduce_scatter x1, waiting for transfers between devices, local(): lax.psum_scatter(parts, OWNER_AXES, scatter_dimension=0, tiled=True)  47.6 us
    all_gather x1, waiting for transfers between devices, local(): gathered = lax.all_gather(normed, 'tensor', axis=0, tiled=True)  47.4 us
    reduce_scatter x1, waiting for transfers between devices, local(): lax.psum_scatter(jnp.dot(scaled, project_weight, preferred_element_type=j...  41.3 us
    psum x1, blocking collectives, local(): inverse = lax.rsqrt(lax.psum(squares, 'tensor') / teacher_width + EPSILON)  21.5 us
    all_gather x1, waiting for transfers between devices, local(): act_all = lax.all_gather(activated, OWNER_AXES, axis=0, tiled=True)  18.4 us
    another operation x4, local copies, waits for them, and re-layouts, local(): jnp.stack([gate_part.astype(jnp.bfloat16).reshape(owners, -1, hidden), up...  17.2 us
  transfers between devices with their start and end apart: 15, of which 14 were waited for; matrix products, arithmetic and copies ran while one was open for 7% of the time, Pallas kernels for 0%

profile of v1, /device:TPU:0, one launch (start us, length us, event | category | flops | bytes accessed | tf_op | source)
XLA Modules:
  0.0 396.3 jit_solution(5200581541820296720)
XLA Ops:
  7.2 1.2 multiply_reduce_fusion
  8.4 1.0 reshape.158
  9.4 0.7 eq.52
  10.2 0.8 select_reduce_fusion
  11.0 0.7 fusion.36
  11.7 0.1 select_n.85
  11.8 0.7 convert_bitcast_fusion
  12.5 0.1 tile.13
  12.6 0.1 copy.50
  12.8 0.7 pad_maximum_fusion.1
  13.5 4.2 %all-to-all-start = ((bf16[4,32,1024]{2,1,0:T(8,128)(2,1)}), bf16[4,32,1024]{2,1,0:T(8,128)(2,1)S(1)}, u32[]{:S(2)}, u32[]{:S(2)}) async-start(bf16[4,32,1024]{2,1,0:T(8,128)(2,1)} %pad_maximum_fusion.1), calls=%async_computation | async-start | bytes 524288 | tf_op jit(solution)/shard_map/all_to_all | solution.py:33
  17.8 0.8 dynamic_slice.30
  18.5 5.2 %all-to-all-done = bf16[4,32,1024]{2,1,0:T(8,128)(2,1)S(1)} async-done(((bf16[4,32,1024]{2,1,0:T(8,128)(2,1)}), bf16[4,32,1024]{2,1,0:T(8,128)(2,1)S(1)}, u32[]{:S(2)}, u32[]{:S(2)}) %all-to-all-start) | async-done | bytes 262176 | tf_op jit(solution)/shard_map/all_to_all | solution.py:33
  23.8 0.2 slice_reduce_fusion
  24.0 0.1 add.174
  24.1 0.8 fusion.8
  25.0 47.4 %all-gather.3.cloned.1.call-done = bf16[1024,896]{1,0:T(8,128)(2,1)} async-done(((bf16[128,896]{1,0:T(8,128)(2,1)}), bf16[1024,896]{1,0:T(8,128)(2,1)}) %all-gather.3.cloned.1.call-update) | async-done | bytes 1835024 | tf_op jit(solution)/shard_map/all_gather | solution.py:116
  72.4 5.5 %convolution_convert_fusion.1 = bf16[1024,1184]{0,1:T(8,128)(2,1)} fusion(bf16[1024,896]{1,0:T(8,128)(2,1)} %all-gather.3.cloned.1.call-done, bf16[896,1184]{0,1:T(8,128)(2,1)S(1)} %copy-done), kind=kOutput, calls=%fused_computation.9 | convolution fusion | flops 2173861888 | bytes 6381568 | tf_op jit(solution)/shard_map/dot_general | solution.py:131
  77.9 5.7 %stack_reshape.7 = bf16[4,1,256,1184]{2,0,3,1:T(4,128)(2,1)} reshape(bf16[1024,1184]{0,1:T(8,128)(2,1)} %convolution_convert_fusion.1) | data formatting | bytes 4849664 | tf_op jit(solution)/shard_map/stack;reshape | solution.py:132
  83.6 3.6 copy.45
  87.2 4.0 %convolution_convert_fusion.2 = bf16[1024,1184]{0,1:T(8,128)(2,1)} fusion(bf16[1024,896]{1,0:T(8,128)(2,1)S(1)} %copy-done.6, bf16[896,1184]{0,1:T(8,128)(2,1)S(1)} %copy-done.5), kind=kOutput, calls=%fused_computation.10 | convolution fusion | flops 2173861888 | bytes 6381568 | tf_op jit(solution)/shard_map/dot_general | solution.py:130
  91.2 5.7 %stack_reshape.6 = bf16[4,1,256,1184]{2,0,3,1:T(4,128)(2,1)} reshape(bf16[1024,1184]{0,1:T(8,128)(2,1)} %convolution_convert_fusion.2) | data formatting | bytes 4849664 | tf_op jit(solution)/shard_map/stack;reshape | solution.py:132
  96.9 2.1 copy.44
  99.1 0.3 copy-done.2
  99.3 2.6 pad_maximum_fusion
  102.0 47.6 %reduce-scatter.4.cloned.1.call-done = bf16[1,2,256,1184]{2,3,1,0:T(8,128)(2,1)} async-done(((bf16[4,2,256,1184]{2,3,1,0:T(8,128)(2,1)}), bf16[1,2,256,1184]{2,3,1,0:T(8,128)(2,1)}) %reduce-scatter.4.cloned.1.call-update) | async-done | bytes 1212432 | tf_op jit(solution)/shard_map/reduce_scatter | solution.py:139
  149.6 1.4 convert_element_type.93
  151.1 1.2 fusion.2
  152.3 6.4 %convolution_convert_fusion = bf16[256,3584]{1,0:T(8,128)(2,1)} fusion(bf16[1024,3584]{1,0:T(8,128)(2,1)} %param.14, bf16[256,1024]{1,0:T(8,128)(2,1)S(1)} %copy-done.4, f32[1024]{0:T(1024)S(1)} %copy-done.7), kind=kOutput, calls=%fused_computation | convolution fusion | flops 1880752128 | bytes 9703424 | tf_op jit(solution)/shard_map/dot_general | solution.py:122
  158.8 18.4 %all-gather.5.cloned.1.call-done = bf16[1024,1184]{0,1:T(8,128)(2,1)} async-done(((bf16[256,1184]{0,1:T(8,128)(2,1)}), bf16[1024,1184]{0,1:T(8,128)(2,1)}) %all-gather.5.cloned.1.call-update) | async-done | bytes 2424848 | tf_op jit(solution)/shard_map/all_gather | solution.py:141
  177.1 6.5 %convolution_convert_fusion.3 = bf16[1024,896]{1,0:T(8,128)(2,1)} fusion(bf16[1024,1184]{0,1:T(8,128)(2,1)} %all-gather.5.cloned.1.call-done, bf16[1184,896]{1,0:T(8,128)(2,1)} %param.19), kind=kOutput, calls=%fused_computation.11 | convolution fusion | flops 2173566976 | bytes 6381568 | tf_op jit(solution)/shard_map/dot_general | solution.py:142
  183.8 0.2 fusion.4
  184.0 21.5 %psum.7 = f32[256]{0:T(256)S(1)} all-reduce(f32[256]{0:T(256)S(1)} %fusion.4), channel_id=1, replica_groups=mesh['group'=2,'dp'=2,'tensor'=8] {'tensor'}, use_global_device_ids=true, to_apply=%region_8.9 | all-reduce | flops 256 | bytes 2048 | tf_op jit(solution)/shard_map/psum | solution.py:120
  205.6 0.3 fusion.26
  205.9 41.3 %reduce-scatter.8.cloned.1.call-done = bf16[32,3584]{1,0:T(8,128)(2,1)} async-done(((bf16[256,3584]{1,0:T(8,128)(2,1)}), bf16[32,3584]{1,0:T(8,128)(2,1)}) %reduce-scatter.8.cloned.1.call-update) | async-done | bytes 229392 | tf_op jit(solution)/shard_map/reduce_scatter | solution.py:121
  247.2 1.0 multiply_convert_fusion
  248.3 0.7 copy.55
  249.0 3.6 all-to-all-start.2
  252.6 0.1 mul.127
  252.7 0.2 select_reduce_fusion.1
  253.0 5.0 %all-to-all-done.2 = bf16[4,32,896]{2,1,0:T(8,128)(2,1)S(1)} async-done(((bf16[4,32,896]{2,1,0:T(8,128)(2,1)}), bf16[4,32,896]{2,1,0:T(8,128)(2,1)S(1)}, u32[]{:S(2)}, u32[]{:S(2)}) %all-to-all-start.2) | async-done | bytes 229408 | tf_op jit(solution)/shard_map/all_to_all | solution.py:33
  258.0 58.7 %reduce-scatter.6.cloned.1.call-done = bf16[128,896]{1,0:T(8,128)(2,1)} async-done(((bf16[1024,896]{1,0:T(8,128)(2,1)}), bf16[128,896]{1,0:T(8,128)(2,1)}) %reduce-scatter.6.cloned.1.call-update) | async-done | bytes 229392 | tf_op jit(solution)/shard_map/reduce_scatter | solution.py:143
  316.7 1.1 fusion.11
  317.8 0.4 fusion
  318.2 0.8 copy.54
  319.0 3.5 all-to-all-start.1
  322.5 0.9 collective-permute-start
  323.4 1.7 fusion.20
  325.0 8.1 %collective-permute-done = bf16[128,896]{1,0:T(8,128)(2,1)S(1)} collective-permute-done((bf16[128,896]{1,0:T(8,128)(2,1)S(1)}, bf16[128,896]{1,0:T(8,128)(2,1)S(1)}, u32[]{:S(2)}, u32[]{:S(2)}) %collective-permute-start) | collective-permute-done | bytes 229408 | tf_op jit(solution)/shard_map/ppermute | solution.py:24
  333.2 3.7 convolution_add_fusion.6
  336.9 0.4 copy.47
  337.2 0.9 reshape.162
  338.2 4.8 %collective-permute-done.1 = bf16[128,896]{1,0:T(8,128)(2,1)S(1)} collective-permute-done((bf16[128,896]{1,0:T(8,128)(2,1)S(1)}, bf16[128,896]{1,0:T(8,128)(2,1)S(1)}, u32[]{:S(2)}, u32[]{:S(2)}) %collective-permute-start.1) | collective-permute-done | bytes 229408 | tf_op jit(solution)/shard_map/ppermute | solution.py:24
  342.9 3.0 convolution_add_fusion.5
  345.9 5.9 %collective-permute-done.2 = bf16[128,896]{1,0:T(8,128)(2,1)S(1)} collective-permute-done((bf16[128,896]{1,0:T(8,128)(2,1)S(1)}, bf16[128,896]{1,0:T(8,128)(2,1)S(1)}, u32[]{:S(2)}, u32[]{:S(2)}) %collective-permute-start.2) | collective-permute-done | bytes 229408 | tf_op jit(solution)/shard_map/ppermute | solution.py:24
  351.8 0.7 convolution_add_fusion.4
  352.6 8.0 %collective-permute-done.3 = bf16[128,896]{1,0:T(8,128)(2,1)S(1)} collective-permute-done((bf16[128,896]{1,0:T(8,128)(2,1)S(1)}, bf16[128,896]{1,0:T(8,128)(2,1)S(1)}, u32[]{:S(2)}, u32[]{:S(2)}) %collective-permute-start.3) | collective-permute-done | bytes 229408 | tf_op jit(solution)/shard_map/ppermute | solution.py:24
  360.6 0.7 convolution_add_fusion.3
  361.3 8.0 %collective-permute-done.4 = bf16[128,896]{1,0:T(8,128)(2,1)S(1)} collective-permute-done((bf16[128,896]{1,0:T(8,128)(2,1)S(1)}, bf16[128,896]{1,0:T(8,128)(2,1)S(1)}, u32[]{:S(2)}, u32[]{:S(2)}) %collective-permute-start.4) | collective-permute-done | bytes 229408 | tf_op jit(solution)/shard_map/ppermute | solution.py:24
  369.3 0.7 convolution_add_fusion.2
  370.0 8.3 %collective-permute-done.5 = bf16[128,896]{1,0:T(8,128)(2,1)S(1)} collective-permute-done((bf16[128,896]{1,0:T(8,128)(2,1)S(1)}, bf16[128,896]{1,0:T(8,128)(2,1)S(1)}, u32[]{:S(2)}, u32[]{:S(2)}) %collective-permute-start.5) | collective-permute-done | bytes 229408 | tf_op jit(solution)/shard_map/ppermute | solution.py:24
  378.3 0.7 convolution_add_fusion.1
  379.0 8.0 %collective-permute-done.6 = bf16[128,896]{1,0:T(8,128)(2,1)S(1)} collective-permute-done((bf16[128,896]{1,0:T(8,128)(2,1)S(1)}, bf16[128,896]{1,0:T(8,128)(2,1)S(1)}, u32[]{:S(2)}, u32[]{:S(2)}) %collective-permute-start.6) | collective-permute-done | bytes 229408 | tf_op jit(solution)/shard_map/ppermute | solution.py:24
  387.0 2.7 convolution_add_fusion
  (46 shorter events, 0.6 us)
Async XLA Ops:
  7.2 65.3 %copy-start = (bf16[896,1184]{0,1:T(8,128)(2,1)S(1)}, bf16[896,1184]{0,1:T(8,128)(2,1)}, u32[]{:S(2)}) copy-start(bf16[896,1184]{0,1:T(8,128)(2,1)} %param.18) | copy-start | bytes 6365188
  13.5 10.2 %all-to-all-start = ((bf16[4,32,1024]{2,1,0:T(8,128)(2,1)}), bf16[4,32,1024]{2,1,0:T(8,128)(2,1)S(1)}, u32[]{:S(2)}, u32[]{:S(2)}) async-start(bf16[4,32,1024]{2,1,0:T(8,128)(2,1)} %pad_maximum_fusion.1), calls=%async_computation | async-start | bytes 524288 | tf_op jit(solution)/shard_map/all_to_all | solution.py:33
  17.8 54.7 %all-gather.3.cloned.1.call-start = ((), (), s32[]{:S(2)}) async-start(), calls=%async_computation.6 | async-start | bytes 2064384 | tf_op jit(solution)/shard_map/all_gather | solution.py:116
  24.9 124.6 %reduce-scatter.4.cloned.1.call-start = ((), (), s32[]{:S(2)}) async-start(), calls=%async_computation.7 | async-start | bytes 6062080 | tf_op jit(solution)/shard_map/reduce_scatter | solution.py:139
  83.6 3.6 copy-start.5
  83.6 3.6 copy-start.6
  96.9 2.4 copy-start.2
  101.9 75.2 %all-gather.5.cloned.1.call-start = ((), (), s32[]{:S(2)}) async-start(), calls=%async_computation.8 | async-start | bytes 3031040 | tf_op jit(solution)/shard_map/all_gather | solution.py:141
  151.0 1.3 copy-start.4
  151.0 1.3 copy-start.7
  152.3 94.9 %reduce-scatter.8.cloned.1.call-start = ((), (), s32[]{:S(2)}) async-start(), calls=%async_computation.10 | async-start | bytes 2064384 | tf_op jit(solution)/shard_map/reduce_scatter | solution.py:121
  158.7 158.0 %reduce-scatter.6.cloned.1.call-start = ((), (), s32[]{:S(2)}) async-start(), calls=%async_computation.9 | async-start | bytes 2064384 | tf_op jit(solution)/shard_map/reduce_scatter | solution.py:143
  249.0 9.0 %all-to-all-start.2 = ((bf16[4,32,896]{2,1,0:T(8,128)(2,1)}), bf16[4,32,896]{2,1,0:T(8,128)(2,1)S(1)}, u32[]{:S(2)}, u32[]{:S(2)}) async-start(bf16[4,32,896]{2,1,0:T(8,128)(2,1)} %bitcast.70), calls=%async_computation.5 | async-start | bytes 458752 | tf_op jit(solution)/shard_map/all_to_all | solution.py:33
  319.0 17.9 %all-to-all-start.1 = ((bf16[4,2,32,896]{3,2,1,0:T(8,128)(2,1)}), bf16[4,2,32,896]{3,2,1,0:T(8,128)(2,1)S(1)}, u32[]{:S(2)}, u32[]{:S(2)}) async-start(bf16[4,2,32,896]{3,2,1,0:T(8,128)(2,1)} %bitcast.68), calls=%async_computation.3 | async-start | bytes 917504 | tf_op jit(solution)/shard_map/all_to_all | solution.py:33
  322.5 10.7 %collective-permute-start = (bf16[128,896]{1,0:T(8,128)(2,1)S(1)}, bf16[128,896]{1,0:T(8,128)(2,1)S(1)}, u32[]{:S(2)}, u32[]{:S(2)}) collective-permute-start(bf16[128,896]{1,0:T(8,128)(2,1)S(1)} %get-tuple-element.6), channel_id=1, source_target_pairs={{0,1},{1,2},{2,3},{3,4},{4,5},{5,6},{6,7},{7,0},{8,9},{9,10},{10,1... | collective-permute-start | bytes 688136 | tf_op jit(solution)/shard_map/ppermute | solution.py:24
  333.2 9.8 %collective-permute-start.1 = (bf16[128,896]{1,0:T(8,128)(2,1)S(1)}, bf16[128,896]{1,0:T(8,128)(2,1)S(1)}, u32[]{:S(2)}, u32[]{:S(2)}) collective-permute-start(bf16[128,896]{1,0:T(8,128)(2,1)S(1)} %collective-permute-done), channel_id=1, source_target_pairs={{0,1},{1,2},{2,3},{3,4},{4,5},{5,6},{6,7},{7,0},{8,9},{9,10},{10,1... | collective-permute-start | bytes 688136 | tf_op jit(solution)/shard_map/ppermute | solution.py:24
  338.2 13.7 %copy-start.3 = (bf16[1024,1184]{0,1:T(8,128)(2,1)S(1)}, bf16[1024,1184]{0,1:T(8,128)(2,1)}, u32[]{:S(2)}) copy-start(bf16[1024,1184]{0,1:T(8,128)(2,1)} %all-gather.5.cloned.1.call-done) | copy-start | bytes 7274500
  342.9 8.9 %collective-permute-start.2 = (bf16[128,896]{1,0:T(8,128)(2,1)S(1)}, bf16[128,896]{1,0:T(8,128)(2,1)S(1)}, u32[]{:S(2)}, u32[]{:S(2)}) collective-permute-start(bf16[128,896]{1,0:T(8,128)(2,1)S(1)} %collective-permute-done.1), channel_id=1, source_target_pairs={{0,1},{1,2},{2,3},{3,4},{4,5},{5,6},{6,7},{7,0},{8,9},{9,10},{10,1... | collective-permute-start | bytes 688136 | tf_op jit(solution)/shard_map/ppermute | solution.py:24
  351.8 8.7 %collective-permute-start.3 = (bf16[128,896]{1,0:T(8,128)(2,1)S(1)}, bf16[128,896]{1,0:T(8,128)(2,1)S(1)}, u32[]{:S(2)}, u32[]{:S(2)}) collective-permute-start(bf16[128,896]{1,0:T(8,128)(2,1)S(1)} %collective-permute-done.2), channel_id=1, source_target_pairs={{0,1},{1,2},{2,3},{3,4},{4,5},{5,6},{6,7},{7,0},{8,9},{9,10},{10,1... | collective-permute-start | bytes 688136 | tf_op jit(solution)/shard_map/ppermute | solution.py:24
  360.6 8.7 %collective-permute-start.4 = (bf16[128,896]{1,0:T(8,128)(2,1)S(1)}, bf16[128,896]{1,0:T(8,128)(2,1)S(1)}, u32[]{:S(2)}, u32[]{:S(2)}) collective-permute-start(bf16[128,896]{1,0:T(8,128)(2,1)S(1)} %collective-permute-done.3), channel_id=1, source_target_pairs={{0,1},{1,2},{2,3},{3,4},{4,5},{5,6},{6,7},{7,0},{8,9},{9,10},{10,1... | collective-permute-start | bytes 688136 | tf_op jit(solution)/shard_map/ppermute | solution.py:24
  369.3 9.0 %collective-permute-start.5 = (bf16[128,896]{1,0:T(8,128)(2,1)S(1)}, bf16[128,896]{1,0:T(8,128)(2,1)S(1)}, u32[]{:S(2)}, u32[]{:S(2)}) collective-permute-start(bf16[128,896]{1,0:T(8,128)(2,1)S(1)} %collective-permute-done.4), channel_id=1, source_target_pairs={{0,1},{1,2},{2,3},{3,4},{4,5},{5,6},{6,7},{7,0},{8,9},{9,10},{10,1... | collective-permute-start | bytes 688136 | tf_op jit(solution)/shard_map/ppermute | solution.py:24
  378.3 8.7 %collective-permute-start.6 = (bf16[128,896]{1,0:T(8,128)(2,1)S(1)}, bf16[128,896]{1,0:T(8,128)(2,1)S(1)}, u32[]{:S(2)}, u32[]{:S(2)}) collective-permute-start(bf16[128,896]{1,0:T(8,128)(2,1)S(1)} %collective-permute-done.5), channel_id=1, source_target_pairs={{0,1},{1,2},{2,3},{3,4},{4,5},{5,6},{6,7},{7,0},{8,9},{9,10},{10,1... | collective-permute-start | bytes 688136 | tf_op jit(solution)/shard_map/ppermute | solution.py:24
  378.3 11.5 %copy-start.1 = (bf16[896,1184]{0,1:T(8,128)(2,1)S(1)}, bf16[896,1184]{0,1:T(8,128)(2,1)}, u32[]{:S(2)}) copy-start(bf16[896,1184]{0,1:T(8,128)(2,1)} %param.18) | copy-start | bytes 6365188
Sparse Core Ops, SparseCore 0:
  25.1 47.3 all-gather.2
  102.0 47.4 reduce-scatter.3
  152.4 24.6 all-gather.4
  180.4 66.7 reduce-scatter.7
  251.1 65.5 reduce-scatter.5
